TPU v7x, 256 devices: a whole 4x4x8 slice. The times are simulated.
256 devices in a mesh: dp: 32 (over x, z_lo, core), tensor: 8 (over y, z_hi).
Axes of the slice: x: 4, y: 4, z: 8 (z_hi: 2, z_lo: 4; z = z_hi * 4 + z_lo), core: 2. Of those that a mesh axis runs over, the one named last changes fastest.
Arguments:
- inputs: bfloat16 [32, 1024, 4096], P('dp', 'tensor'), may hold values from -40 to 40
- query_states: bfloat16 [32, 1024, 3072], P('dp', None, 'tensor'), may hold values from -4.5 to 4.5
- key_states: bfloat16 [32, 1024, 1024], P('dp', None, 'tensor'), may hold values from -4.5 to 4.5
- saved_value_states: bfloat16 [32, 1024, 1024], P('dp', None, 'tensor'), may hold values from -4.5 to 4.5
- head_cotangent: bfloat16 [32, 1024, 3072], P('dp', None, 'tensor'), may hold values from -40 to 40
- query_weight: bfloat16 [4096, 3072], P('dp', 'tensor'), may hold values from -0.09375 to 0.09375
- key_matrix: bfloat16 [4096, 1024], P('dp', 'tensor'), may hold values from -0.09375 to 0.09375
- value_matrix: bfloat16 [4096, 1024], P('dp', 'tensor'), may hold values from -0.09375 to 0.09375
- query_momentum: float32 [4096, 3072], P('dp', 'tensor'), may hold values from -6 to 6
- key_prior_momentum: float32 [4096, 1024], P('dp', 'tensor'), may hold values from -6 to 6
- value_prior_momentum: float32 [4096, 1024], P('dp', 'tensor'), may hold values from -6 to 6
Outputs:
- input_gradient: bfloat16 [32, 1024, 4096], P('dp', 'tensor')
- query_velocity: float32 [4096, 3072], P('dp', 'tensor')
- key_velocity: float32 [4096, 1024], P('dp', 'tensor')
- value_velocity: float32 [4096, 1024], P('dp', 'tensor')
All inputs are finite; a program needn't handle non-finite values.
Results may differ from a plain program's by a relative error of at most 0.019.
Values may be sent and summed in bfloat16 or wider, within the bound.
A program may use at most 128 MiB of HBM per device.

v0:
```python
import functools
import math

import jax
import jax.numpy as jnp
from jax import lax
from jax.sharding import Mesh
from jax.sharding import PartitionSpec as P

MODEL_FEATURES = 4096
QUERY_HEADS = 24
KEY_VALUE_HEADS = 8
HEAD_SIZE = 128
DP = ("dp_0", "dp_1", "dp_2")
TENSOR = ("tensor_0", "tensor_1")
DP_TENSOR = ("dp_0", "dp_1", "dp_2", "tensor_0", "tensor_1")


def summed_rows(terms, axes):
    so_far = terms.astype(jnp.bfloat16)
    for axis in axes:
        so_far = lax.psum_scatter(so_far, axis, scatter_dimension=0, tiled=True)
    return so_far.astype(jnp.float32)


def in_blocks(value, dim, length):
    before, after = (value.shape[:dim], value.shape[dim + 1 :])
    return jnp.moveaxis(value.reshape(*before, length, -1, *after), dim, 0)


def scatter_pairs(value, chips, core, dim):
    sizes = (lax.axis_size(chips), lax.axis_size(core))
    parts = in_blocks(value, dim, sizes[0] * sizes[1])
    inside = parts.shape[1:]
    parts = parts.reshape(*sizes, *inside).swapaxes(0, 1).reshape(-1, *inside)
    parts = lax.psum_scatter(parts, core, scatter_dimension=0, tiled=True)
    return lax.psum_scatter(parts, chips, scatter_dimension=0, tiled=True)[0]


def over_axes(value, axes):
    return functools.reduce(lax.psum, axes, value)


def heads_backward(query_row_set, key_rows, value_rows, cotangent_rows):
    token_length = query_row_set.shape[0]
    kv_heads = key_rows.shape[1] // HEAD_SIZE
    group_width = query_row_set.shape[1] // HEAD_SIZE // kv_heads
    scaling = 1.0 / math.sqrt(HEAD_SIZE)
    query_quad = query_row_set.reshape(token_length, kv_heads, group_width, HEAD_SIZE)
    cotangent_quad = cotangent_rows.reshape(token_length, kv_heads, group_width, HEAD_SIZE)
    key_triple = key_rows.reshape(token_length, kv_heads, HEAD_SIZE)
    value_triple = value_rows.reshape(token_length, kv_heads, HEAD_SIZE)
    block_rows = min(token_length, 512)
    key_sums = jnp.zeros((token_length, kv_heads, HEAD_SIZE), jnp.float32)
    value_sums = jnp.zeros((token_length, kv_heads, HEAD_SIZE), jnp.float32)
    query_blocks = []
    for row_start in range(0, token_length, block_rows):
        row_end = row_start + block_rows
        query_block = query_quad[row_start:row_end]
        cotangent_block = cotangent_quad[row_start:row_end]
        key_block = key_triple[:row_end]
        value_block = value_triple[:row_end]
        scores = (
            jnp.einsum("ihgd,jhd->hgij", query_block, key_block, preferred_element_type=jnp.float32)
            * scaling
        )
        query_index = row_start + lax.broadcasted_iota(jnp.int32, (block_rows, row_end), 0)
        key_index = lax.broadcasted_iota(jnp.int32, (block_rows, row_end), 1)
        scores = jnp.where(query_index >= key_index, scores, -jnp.inf)
        maximum = jnp.max(scores, axis=-1, keepdims=True)
        exponent = jnp.exp(scores - maximum)
        softmax_rows = exponent / jnp.sum(exponent, axis=-1, keepdims=True)
        softmax_reduced = softmax_rows.astype(jnp.bfloat16)
        grad_softmax = jnp.einsum(
            "ihgd,jhd->hgij", cotangent_block, value_block, preferred_element_type=jnp.float32
        )
        row_delta = jnp.sum(softmax_rows * grad_softmax, axis=-1, keepdims=True)
        score_gradient = (softmax_rows * (grad_softmax - row_delta) * scaling).astype(jnp.bfloat16)
        query_blocks.append(
            jnp.einsum(
                "hgij,jhd->ihgd", score_gradient, key_block, preferred_element_type=jnp.float32
            ).astype(jnp.bfloat16)
        )
        key_sums = key_sums.at[:row_end].add(
            jnp.einsum(
                "xfwo,wxfp->oxp", score_gradient, query_block, preferred_element_type=jnp.float32
            )
        )
        value_sums = value_sums.at[:row_end].add(
            jnp.einsum(
                "xfwo,wxfp->oxp",
                softmax_reduced,
                cotangent_block,
                preferred_element_type=jnp.float32,
            )
        )
    grad_query = jnp.concatenate(query_blocks, axis=0).reshape(token_length, -1)
    key_gradient = key_sums.astype(jnp.bfloat16).reshape(token_length, -1)
    value_gradient = value_sums.astype(jnp.bfloat16).reshape(token_length, -1)
    return (grad_query, key_gradient, value_gradient)


def local(
    inputs,
    query_states,
    key_states,
    saved_value_states,
    head_cotangent,
    query_weight,
    key_matrix,
    value_matrix,
    query_momentum,
    key_prior_momentum,
    value_prior_momentum,
):
    query_cols = query_weight.shape[1]
    pair_cols = key_matrix.shape[1]
    local_weights = jnp.concatenate((query_weight, key_matrix, value_matrix), axis=1)
    all_weights = lax.all_gather(local_weights, DP, axis=0, tiled=True)
    gathered = lax.all_gather(inputs, TENSOR, axis=1, tiled=True)[0]
    grad_query, key_gradient, value_gradient = heads_backward(
        query_states[0], key_states[0], saved_value_states[0], head_cotangent[0]
    )
    local_grads = jnp.concatenate((grad_query, key_gradient, value_gradient), axis=1)
    grad_inputs = summed_rows(
        lax.dot_general(
            local_grads, all_weights, (((1,), (1,)), ((), ())), preferred_element_type=jnp.float32
        ),
        TENSOR,
    ).astype(jnp.bfloat16)[None]
    summed = scatter_pairs(
        lax.dot_general(
            gathered, local_grads, (((0,), (0,)), ((), ())), preferred_element_type=jnp.float32
        ).astype(jnp.bfloat16),
        ("dp_0", "dp_1"),
        "dp_2",
        0,
    ).astype(jnp.float32)
    local_squares = jnp.sum(summed * summed)
    squared_total = over_axes(local_squares, DP_TENSOR)
    summed, squared_total = (summed, squared_total)
    grad_w_query = summed[:, :query_cols]
    grad_w_key = summed[:, query_cols : query_cols + pair_cols]
    grad_w_value = summed[:, query_cols + pair_cols :]
    root_mean_square = jnp.sqrt(
        squared_total / (MODEL_FEATURES * (QUERY_HEADS + 2 * KEY_VALUE_HEADS) * HEAD_SIZE)
    )
    factor = 1.0 / jnp.maximum(root_mean_square, 1.0)
    query_velocity = 0.9 * query_momentum + factor * grad_w_query
    key_velocity = 0.9 * key_prior_momentum + factor * grad_w_key
    value_velocity = 0.9 * value_prior_momentum + factor * grad_w_value
    return (grad_inputs, query_velocity, key_velocity, value_velocity)


def solution(mesh):
    torus = Mesh(
        mesh.devices.reshape(4, 4, 2, 4, 2), ("dp_0", "dp_1", "dp_2", "tensor_0", "tensor_1")
    )
    in_specs = (
        P(DP, TENSOR, None),
        P(DP, None, TENSOR),
        P(DP, None, TENSOR),
        P(DP, None, TENSOR),
        P(DP, None, TENSOR),
        P(DP, TENSOR),
        P(DP, TENSOR),
        P(DP, TENSOR),
        P(DP, TENSOR),
        P(DP, TENSOR),
        P(DP, TENSOR),
    )
    out_specs = (P(DP, TENSOR, None), P(DP, TENSOR), P(DP, TENSOR), P(DP, TENSOR))
    return jax.shard_map(local, mesh=torus, in_specs=in_specs, out_specs=out_specs, check_vma=False)
```

profile of v0, /device:TPU:2, one launch (start us, length us, event | category | flops | bytes accessed | tf_op | source)
XLA Modules:
  0.0 522.1 jit_solution(1781545789041277618)
XLA Ops:
  8.0 1.6 pad_maximum_fusion.4
  9.6 1.2 fusion.74
  14.9 1.8 fusion.25
  17.4 1.2 fusion.18
  18.6 1.1 fusion.27
  20.9 1.3 fusion.14
  22.2 1.4 fusion.13
  23.6 2.6 fusion.5
  26.2 2.2 fusion.15
  28.5 1.7 copy-done.1
  30.2 1.0 fusion.39
  32.1 2.3 copy.38
  34.5 2.1 convolution_bitcast_fusion.1
  36.6 3.9 fusion.47
  40.6 1.1 fusion.48
  42.3 2.1 fusion.44
  44.5 142.0 %all-gather.5.cloned.1.call-done = bf16[1,1024,4096]{2,1,0:T(8,128)(2,1)} async-done(((bf16[1,128,4096]{2,1,0:T(8,128)(2,1)}), bf16[1,1024,4096]{2,1,0:T(8,128)(2,1)}) %all-gather.5.cloned.1.call-update) | async-done | bytes 8388624 | tf_op jit(solution)/shard_map/all_gather | solution.py:120
  186.5 11.7 %fusion.9 = bf16[4096,640]{0,1:T(8,128)(2,1)} fusion(bf16[1,1024,4096]{2,1,0:T(8,128)(2,1)} %all-gather.5.cloned.1.call-done, bf16[1024,128]{0,1:T(8,128)(2,1)S(1)} %fusion.44, bf16[1024,128]{0,1:T(8,128)(2,1)S(1)} %copy-done.17, bf16[1024,384]{0,1:T(8,128)(2,1)S(1)} %bitcast.225), kind=kOutput, calls=%fused_computation.12 | convolution fusion | flops 5375262720 | bytes 14942208 | tf_op jit(solution)/shard_map/dot_general | solution.py:132
  198.2 9.4 %reshape_reshape.3 = bf16[16,2,128,640]{2,1,0,3:T(2,128)(2,1)} reshape(bf16[4096,640]{0,1:T(8,128)(2,1)} %fusion.9) | data formatting | bytes 10485760 | tf_op jit(solution)/shard_map/reshape;reshape | solution.py:35
  207.6 13.8 %copy.43 = bf16[2,16,128,640]{3,2,1,0:T(8,128)(2,1)} copy(bf16[2,16,128,640]{2,0,1,3:T(2,128)(2,1)} %bitcast.220) | data formatting | bytes 10485760 | tf_op jit(solution)/shard_map/transpose | solution.py:35
  221.5 25.8 %all-gather.3.cloned.1.call-done = bf16[4096,640]{1,0:T(8,128)(2,1)} async-done(((bf16[128,640]{1,0:T(8,128)(2,1)}), bf16[4096,640]{1,0:T(8,128)(2,1)}) %all-gather.3.cloned.1.call-update) | async-done | bytes 5242896 | tf_op jit(solution)/shard_map/all_gather | solution.py:119
  247.3 11.4 %convolution_convert_fusion = bf16[1024,4096]{1,0:T(8,128)(2,1)} fusion(bf16[4096,640]{1,0:T(8,128)(2,1)} %all-gather.3.cloned.1.call-done, bf16[1024,128]{0,1:T(8,128)(2,1)S(1)} %fusion.44, bf16[1024,128]{0,1:T(8,128)(2,1)S(1)} %copy-done.17, bf16[1024,384]{0,1:T(8,128)(2,1)S(1)} %bitcast.226), kind=kOutput, calls=%fused_computation.2 | convolution fusion | flops 5376835584 | bytes 14942208 | tf_op jit(solution)/shard_map/dot_general | solution.py:126
  258.9 8.8 %reduce-scatter.9.cloned.1.call-done = bf16[16,128,640]{2,1,0:T(8,128)(2,1)} async-done(((bf16[32,128,640]{2,1,0:T(8,128)(2,1)}), bf16[16,128,640]{2,1,0:T(8,128)(2,1)}) %reduce-scatter.9.cloned.1.call-update) | async-done | bytes 2621456 | tf_op jit(solution)/shard_map/reduce_scatter | solution.py:36
  267.7 86.8 %reduce-scatter.5.cloned.1.call-done = bf16[256,4096]{1,0:T(8,128)(2,1)} async-done(((bf16[1024,4096]{1,0:T(8,128)(2,1)}), bf16[256,4096]{1,0:T(8,128)(2,1)}) %reduce-scatter.5.cloned.1.call-update) | async-done | bytes 2097168 | tf_op jit(solution)/shard_map/reduce_scatter | solution.py:22
  354.5 88.4 %reduce-scatter.11.cloned.1.call-done = bf16[1,128,640]{2,1,0:T(8,128)(2,1)} async-done(((bf16[16,128,640]{2,1,0:T(8,128)(2,1)}), bf16[1,128,640]{2,1,0:T(8,128)(2,1)}) %reduce-scatter.11.cloned.1.call-update) | async-done | bytes 163856 | tf_op jit(solution)/shard_map/reduce_scatter | solution.py:37
  442.9 1.6 multiply_reduce_fusion
  444.5 16.5 %psum.35 = f32[]{:T(128)} all-reduce(f32[]{:T(128)} %multiply_reduce_fusion), channel_id=1, replica_groups=mesh['dp_0'=4,'dp_1'=4,'dp_2'=2,'tensor_0'=4,'tensor_1'=2] {'dp_0'}, use_global_device_ids=true, to_apply=%region_11.12 | all-reduce | flops 1 | bytes 8 | tf_op jit(solution)/shard_map/psum | solution.py:41
  461.0 11.1 %psum.36 = f32[]{:T(128)} all-reduce(f32[]{:T(128)} %psum.35), channel_id=1, replica_groups=mesh['dp_0'=4,'dp_1'=4,'dp_2'=2,'tensor_0'=4,'tensor_1'=2] {'dp_1'}, use_global_device_ids=true, to_apply=%region_12.13 | all-reduce | flops 1 | bytes 8 | tf_op jit(solution)/shard_map/psum | solution.py:41
  472.1 3.1 psum.37
  475.2 11.2 %psum.38 = f32[]{:T(128)} all-reduce(f32[]{:T(128)} %psum.37), channel_id=1, replica_groups=mesh['dp_0'=4,'dp_1'=4,'dp_2'=2,'tensor_0'=4,'tensor_1'=2] {'tensor_0'}, use_global_device_ids=true, to_apply=%region_14.15 | all-reduce | flops 1 | bytes 8 | tf_op jit(solution)/shard_map/psum | solution.py:41
  486.3 9.8 %psum.39 = f32[]{:T(128)} all-reduce(f32[]{:T(128)} %psum.38), channel_id=1, replica_groups=mesh['dp_0'=4,'dp_1'=4,'dp_2'=2,'tensor_0'=4,'tensor_1'=2] {'tensor_1'}, use_global_device_ids=true, to_apply=%region_15.16 | all-reduce | flops 1 | bytes 8 | tf_op jit(solution)/shard_map/psum | solution.py:41
  499.2 16.0 %reduce-scatter.7.cloned.1.call-done = bf16[128,4096]{1,0:T(8,128)(2,1)} async-done(((bf16[256,4096]{1,0:T(8,128)(2,1)}), bf16[128,4096]{1,0:T(8,128)(2,1)}) %reduce-scatter.7.cloned.1.call-update) | async-done | bytes 1048592 | tf_op jit(solution)/shard_map/reduce_scatter | solution.py:22
  (66 shorter events, 10.8 us)
Async XLA Ops:
  7.2 4.6 copy-start.7
  7.2 179.3 %all-gather.5.cloned.1.call-start = ((), (), s32[]{:S(2)}) async-start(), calls=%async_computation.7 | async-start | bytes 9437184 | tf_op jit(solution)/shard_map/all_gather | solution.py:120
  7.9 239.4 %all-gather.3.cloned.1.call-start = ((), (), s32[]{:S(2)}) async-start(), calls=%async_computation.4 | async-start | bytes 5406720 | tf_op jit(solution)/shard_map/all_gather | solution.py:119
  9.6 258.0 %reduce-scatter.9.cloned.1.call-start = ((), (), s32[]{:S(2)}) async-start(), calls=%async_computation.8 | async-start | bytes 7864320 | tf_op jit(solution)/shard_map/reduce_scatter | solution.py:36
  14.8 2.5 copy-start.9
  14.8 2.5 copy-start.16
  18.6 1.1 copy-start.5
  18.6 2.3 copy-start.6
  19.8 1.1 copy-start.2
  20.9 5.3 %copy-start.3 = (pred[512,1024]{0,1:T(8,128)(4,1)}, pred[512,1024]{0,1:T(8,128)(4,1)S(1)}, u32[]{:S(2)}) copy-start(pred[512,1024]{0,1:T(8,128)(4,1)S(1)} %iota_compare_fusion) | copy-start | bytes 1572868
  22.2 4.1 copy-start
  22.2 1.4 copy-start.11
  28.5 1.7 copy-start.1
  36.6 4.0 copy-start.10
  36.6 5.1 slice-start
  40.5 1.6 slice-start.1
  40.6 1.7 copy-start.4
  40.6 1.8 copy-start.12
  42.3 144.1 %copy-start.8 = (bf16[1024,1,3,128]{0,3,2,1:T(8,128)(2,1)S(1)}, bf16[1024,1,3,128]{0,3,2,1:T(8,128)(2,1)}, u32[]{:S(2)}) copy-start(bf16[1024,1,3,128]{0,3,2,1:T(8,128)(2,1)} %copy.38) | copy-start | bytes 2359300
  42.3 144.1 %copy-start.17 = (bf16[1024,128]{0,1:T(8,128)(2,1)S(1)}, bf16[1024,128]{0,1:T(8,128)(2,1)}, u32[]{:S(2)}) copy-start(bf16[1024,128]{0,1:T(8,128)(2,1)} %fusion.47) | copy-start | bytes 786436
  221.5 133.1 %reduce-scatter.5.cloned.1.call-start = ((), (), s32[]{:S(2)}) async-start(), calls=%async_computation.5 | async-start | bytes 10485760 | tf_op jit(solution)/shard_map/reduce_scatter | solution.py:22
  258.8 239.1 %copy-start.14 = (f32[128,128]{1,0:T(8,128)S(1)}, f32[128,128]{1,0:T(8,128)}, u32[]{:S(2)}) copy-start(f32[128,128]{1,0:T(8,128)} %param.33) | copy-start | bytes 196612
  258.8 239.1 %copy-start.15 = (f32[128,128]{1,0:T(8,128)S(1)}, f32[128,128]{1,0:T(8,128)}, u32[]{:S(2)}) copy-start(f32[128,128]{1,0:T(8,128)} %param.32) | copy-start | bytes 196612
  258.8 239.7 %copy-start.13 = (f32[128,384]{1,0:T(8,128)S(1)}, f32[128,384]{1,0:T(8,128)}, u32[]{:S(2)}) copy-start(f32[128,384]{1,0:T(8,128)} %param.31) | copy-start | bytes 589828
  258.8 184.1 %reduce-scatter.11.cloned.1.call-start = ((), (), s32[]{:S(2)}) async-start(), calls=%async_computation.9 | async-start | bytes 2785280 | tf_op jit(solution)/shard_map/reduce_scatter | solution.py:37
  267.6 247.6 %reduce-scatter.7.cloned.1.call-start = ((), (), s32[]{:S(2)}) async-start(), calls=%async_computation.6 | async-start | bytes 3145728 | tf_op jit(solution)/shard_map/reduce_scatter | solution.py:22
Sparse Core Ops, SparseCore 0:
  10.6 175.8 all-gather.4
  188.9 58.3 all-gather.2
  249.9 17.7 reduce-scatter.8
  270.1 84.3 reduce-scatter.4
  356.9 85.9 reduce-scatter.10
  445.9 69.3 reduce-scatter.6
where the time goes:
time: 524 us; the launch traced here: 522 us
  waiting for transfers between devices  369 us (70%)
  blocking collectives  51.6 us (10%)
  matrix products  41 us (8%)
  local copies, waits for them, and re-layouts  33.3 us (6%)
  between operations  15.1 us (3%)
  other arithmetic  12.4 us (2%)
    all_gather x1, waiting for transfers between devices, local(): gathered = lax.all_gather(inputs, TENSOR, axis=1, tiled=True)[0]  142 us
    reduce_scatter x2, waiting for transfers between devices, summed_rows(): so_far = lax.psum_scatter(so_far, axis, scatter_dimension=0, tiled=True)  103 us
    reduce_scatter x1, waiting for transfers between devices, scatter_pairs(): return lax.psum_scatter(parts, chips, scatter_dimension=0, tiled=True)[0]  88.4 us
    psum x5, blocking collectives, over_axes(): return functools.reduce(lax.psum, axes, value)  51.6 us
    all_gather x1, waiting for transfers between devices, local(): all_weights = lax.all_gather(local_weights, DP, axis=0, tiled=True)  25.8 us
    transpose x1, local copies, waits for them, and re-layouts, scatter_pairs(): parts = parts.reshape(*sizes, *inside).swapaxes(0, 1).reshape(-1, *inside)  13.8 us
    dot_general x1, matrix products, local(): lax.dot_general(gathered, local_grads, (((0,), (0,)), ((), ())), preferre...  11.7 us
    dot_general x1, matrix products, local(): lax.dot_general(local_grads, all_weights, (((1,), (1,)), ((), ())), prefe...  11.4 us
  transfers between devices with their start and end apart: 6, of which 6 were waited for; matrix products, arithmetic and copies ran while one was open for 16% of the time, Pallas kernels for 0%

commit v1 on v0

v1 whole, which is shorter than its diff:
```python
import functools
import math

import jax
import jax.numpy as jnp
from jax import lax
from jax.experimental import pallas as pl
from jax.experimental.pallas import tpu as pltpu
from jax.sharding import Mesh
from jax.sharding import PartitionSpec as P

MODEL_FEATURES = 4096
QUERY_HEADS = 24
KEY_VALUE_HEADS = 8
HEAD = 128
DP = ("dp_0", "dp_1", "dp_2")
TENSOR = ("tensor_0", "tensor_1")
AXES = DP + TENSOR
MESH = pl.DeviceIdType.MESH
BF = jnp.bfloat16
F32 = jnp.float32

COLS = 640
ALL = 4 * COLS
QB = 256


def dot(a, b, ca, cb):
    return lax.dot_general(a, b, (((ca,), (cb,)), ((), ())), preferred_element_type=F32)


def lanes(start, size):
    return pl.ds(pl.multiple_of(start, 128), size)


def kernel(
    in_ref, q_ref, k_ref, v_ref, do_ref, wq_ref, wk_ref, wv_ref, mq_ref, mk_ref, mv_ref,
    gx_ref, vq_ref, vk_ref, vv_ref,
    xq, xt, g, w, s_buf, dp_buf, p_buf, ds_buf, dk_acc, dv_acc,
    dw_cs, dw_cr, dw_xs, dw_xr, dw_acc, dw_zs, dw_zr, dw_fin, dw_sw, dw_gr,
    dx_s, dx_r, dx_o, dx_f, sq1, sq2,
    ws_s, ws_r, wz_s, wz_r, wx_s, wx_r, wc_s, wc_r,
    xy_s, xy_r, xz_s, xz_r, go_s, go_r, gf_s, gf_r,
    dc_s, dc_r, dxx_s, dxx_r, dz_s, dz_r, dsw_s, dsw_r,
    ez_s, ez_r, ey_s, ey_r, s1_s, s1_r, s2_s, s2_r,
):
    x, zl, c, y, zh = (lax.axis_index(a) for a in AXES)
    scaling = 1.0 / math.sqrt(HEAD)
    other_c, other_zh = 1 - c, 1 - zh

    def at(dx=0, dl=0, dy=0):
        return (lax.rem(x + dx, 4), lax.rem(zl + dl, 4), c, lax.rem(y + dy, 4), zh)

    swap_dev = (y, zl, c, x, zh)
    core_dev = (x, zl, other_c, y, zh)
    zh_dev = (x, zl, c, y, other_zh)

    def line(dz, dc):
        z = lax.rem(zh * 4 + zl + dz, 8)
        return (x, lax.rem(z, 4), lax.rem(c + dc, 2), y, z // 4)

    plane = [(dx, dy) for dx in range(4) for dy in range(4) if dx or dy]
    column = [(dz, dc) for dz in range(8) for dc in range(2) if dz or dc]

    def send(src, dst, ss, rs, dev):
        return pltpu.make_async_remote_copy(
            src_ref=src, dst_ref=dst, send_sem=ss, recv_sem=rs, device_id=dev, device_id_type=MESH
        )

    barrier = pltpu.get_barrier_semaphore()
    for dx, dy in plane:
        pl.semaphore_signal(barrier, inc=1, device_id=at(dx=dx, dy=dy), device_id_type=MESH)
    for dz, dc in column:
        pl.semaphore_signal(barrier, inc=1, device_id=line(dz, dc), device_id_type=MESH)
    pl.semaphore_wait(barrier, 30)

    w_rows = pl.ds(zl * 128, 128)
    w_parts = ((wq_ref, 0, 384), (wk_ref, 384, 128), (wv_ref, 512, 128))

    def w_swap(n):
        ref, off, size = w_parts[n]
        dst = w.at[c, w_rows, lanes(y * COLS + off, size)]
        return send(ref, dst, ws_s.at[n], ws_r.at[n], swap_dev)

    def w_near(n):
        own = w.at[c, w_rows, lanes(x * COLS, COLS)]
        return send(own, own, wz_s.at[n], wz_r.at[n], at(dl=n + 1))

    def w_far(n):
        own = w.at[c, :, lanes(x * COLS, COLS)]
        return send(own, own, wx_s.at[n], wx_r.at[n], at(dx=n + 1))

    def w_core():
        return send(w.at[c], w.at[c], wc_s, wc_r, core_dev)

    @pl.when(x != y)
    def _():
        for n in range(3):
            w_swap(n).start()

    @pl.when(x == y)
    def _():
        for ref, off, size in w_parts:
            w[c, w_rows, lanes(x * COLS + off, size)] = ref[...]

    def x_rows(dy):
        return pl.ds((2 * lax.rem(y + 4 - dy, 4) + zh) * 128, 128)

    def x_y(n):
        to = lax.rem(y + n + 1, 4)
        return send(
            in_ref.at[0, :, lanes(to * 1024, 1024)], xq.at[x_rows(0)],
            xy_s.at[n], xy_r.at[n], at(dy=n + 1),
        )

    def x_z(n):
        rows = xq.at[x_rows(n)]
        return send(rows, rows, xz_s.at[n], xz_r.at[n], zh_dev)

    own_x = in_ref.at[0, :, lanes(y * 1024, 1024)]
    send(own_x, xq.at[x_rows(0)], xz_s.at[0], xz_r.at[0], zh_dev).start()
    for n in range(3):
        x_y(n).start()
    xq[x_rows(0), :] = own_x[...]

    def g_own(p, d):
        piece = g.at[:, :, :, lanes(y * COLS + p * 128, 128)]
        return send(piece, piece, go_s.at[d, p], go_r.at[d, p], at(dy=1 if d == 0 else 3))

    def g_forward(p, d):
        of = lax.rem(y + (3 if d == 0 else 1), 4)
        half = g.at[2 * d : 2 * d + 2, :, :, lanes(of * COLS + p * 128, 128)]
        return send(half, half, gf_s.at[d, p], gf_r.at[d, p], at(dy=1 if d == 0 else 3))

    dk_acc[...] = jnp.zeros_like(dk_acc)
    dv_acc[...] = jnp.zeros_like(dv_acc)
    causal = lax.broadcasted_iota(jnp.int32, (QB, QB), 0) <= lax.broadcasted_iota(
        jnp.int32, (QB, QB), 1
    )

    def head(h, _):
        cols = lanes(h * HEAD, HEAD)
        for i in range(4):
            rows = pl.ds(i * QB, QB)
            qi, doi = q_ref[0, rows, cols], do_ref[0, rows, cols]
            width = (i + 1) * QB
            top = None
            for j in range(i + 1):
                js = pl.ds(j * QB, QB)
                s = dot(k_ref[0, js, :], qi, 1, 1) * scaling
                if j == i:
                    s = jnp.where(causal, s, -jnp.inf)
                s_buf[js, :] = s
                m = jnp.max(s, axis=0, keepdims=True)
                top = m if top is None else jnp.maximum(top, m)
            total = jnp.zeros((1, QB), F32)
            delta = jnp.zeros((1, QB), F32)
            for j in range(i + 1):
                js = pl.ds(j * QB, QB)
                e = jnp.exp(s_buf[js, :] - top)
                dp = dot(v_ref[0, js, :], doi, 1, 1)
                s_buf[js, :] = e
                dp_buf[js, :] = dp
                total = total + jnp.sum(e, axis=0, keepdims=True)
                delta = delta + jnp.sum(e * dp, axis=0, keepdims=True)
            inverse = 1.0 / total
            delta = delta * inverse
            for j in range(i + 1):
                js = pl.ds(j * QB, QB)
                p = s_buf[js, :] * inverse
                p_buf[js, :] = p.astype(BF)
                ds_buf[js, :] = (p * (dp_buf[js, :] - delta) * scaling).astype(BF)
            dv_acc[:width, :] += dot(p_buf[:width, :], doi, 1, 0)
            dk_acc[:width, :] += dot(ds_buf[:width, :], qi, 1, 0)
            dq = dot(ds_buf[:width, :], k_ref[0, :width, :], 0, 0).astype(BF)
            g[i, :, :, lanes(y * COLS + h * HEAD, HEAD)] = dq.reshape(2, 128, HEAD)
        g_own(h, 0).start()
        g_own(h, 1).start()

        @pl.when(h == 0)
        def _():
            @pl.when(x != y)
            def _():
                for n in range(3):
                    w_swap(n).wait()

            for n in range(3):
                w_near(n).start()

        return 0

    lax.fori_loop(0, 3, head, 0)
    for p, acc in ((3, dk_acc), (4, dv_acc)):
        g[:, :, :, lanes(y * COLS + p * 128, 128)] = acc[...].astype(BF).reshape(4, 2, 128, 128)
        g_own(p, 0).start()
        g_own(p, 1).start()
    for n in range(3):
        x_y(n).wait_recv()
        x_z(n + 1).start()
    for n in range(3):
        w_near(n).wait()
    for n in range(3):
        w_far(n).start()

    def turn(t, _):
        rows = pl.ds(pl.multiple_of(t * 128, 128), 128)
        for b in range(8):
            block = xq[rows, b * 128 : b * 128 + 128]
            xt[b % 2, (b // 2) * 128 : (b // 2) * 128 + 128, lanes(t * 128, 128)] = block.T
        return 0

    for p in range(5):
        for d in range(2):
            g_own(p, d).wait_recv()
            g_forward(p, d).start()
    lax.fori_loop(0, 4, lambda b, _: turn(2 * b + zh, 0), 0)
    for n in range(4):
        x_z(n).wait_recv()
    lax.fori_loop(0, 4, lambda b, _: turn(2 * b + other_zh, 0), 0)
    for n in range(3):
        w_far(n).wait()
    w_core().start()
    for p in range(5):
        for d in range(2):
            g_forward(p, d).wait_recv()

    def d_core(k):
        return send(dw_cs.at[k], dw_cr.at[k], dc_s.at[k], dc_r.at[k], core_dev)

    def d_x(n):
        return send(dw_xs.at[n], dw_xr.at[n], dxx_s.at[n], dxx_r.at[n], at(dx=n + 1))

    def d_z(n):
        return send(dw_zs.at[n], dw_zr.at[n], dz_s.at[n], dz_r.at[n], at(dl=n + 1))

    def d_swap():
        return send(dw_sw, dw_gr, dsw_s, dsw_r, swap_dev)

    def product(half, n):
        k = lax.rem(x + 1 + n, 4)
        rhs = g[:, :, :, lanes(k * COLS, COLS)].reshape(1024, COLS)
        return dot(xt[half], rhs, 1, 0)

    def for_core(n, _):
        dw_cs[n] = product(other_c, n).astype(BF)
        d_core(n).start()
        return 0

    def for_x(n, _):
        part = product(c, n)
        d_core(n).wait_recv()
        part = part + dw_cr[n].astype(F32)

        @pl.when(n < 3)
        def _():
            dw_xs[n] = part.astype(BF)
            d_x(n).start()

        @pl.when(n == 3)
        def _():
            dw_acc[...] = part

        return 0

    lax.fori_loop(0, 4, for_core, 0)
    lax.fori_loop(0, 4, for_x, 0)

    def e_z(n):
        to = lax.rem(y + 1 + n, 4)
        return send(dx_s.at[to], dx_r.at[to], ez_s.at[n], ez_r.at[n], zh_dev)

    def e_y(n):
        dst = gx_ref.at[0, :, lanes(y * 1024, 1024)]
        return send(dx_f.at[n], dst, ey_s.at[n], ey_r.at[n], at(dy=n + 1))

    def back(tokens, half):
        return dot(g[:, tokens].reshape(512, ALL), w[half], 1, 1)

    w_core().wait()
    for half in range(2):
        r = back(other_zh, half).astype(BF).reshape(4, 128, 512)
        for b in range(4):
            dx_s[:, :, b * 256 + half * 128 : b * 256 + half * 128 + 128] = r[:, :, b * 128 : b * 128 + 128]
    for n in range(3):
        e_z(n).start()
    for half in range(2):
        r = back(zh, half).reshape(4, 128, 512)
        for b in range(4):
            dx_o[:, :, b * 256 + half * 128 : b * 256 + half * 128 + 128] = r[:, :, b * 128 : b * 128 + 128]

    def finish(n):
        e_z(n).wait_recv()
        to = lax.rem(y + 1 + n, 4)
        done = (dx_o[to] + dx_r[to].astype(F32)).astype(BF)
        if n < 3:
            dx_f[n] = done
            e_y(n).start()
        else:
            gx_ref[0, :, lanes(y * 1024, 1024)] = done

    finish(0)
    finish(1)
    for n in range(3):
        d_x(n).wait_recv()

    def summed(rows):
        r = dw_acc[rows, :]
        for n in range(3):
            r = r + dw_xr[n, rows, :].astype(F32)
        return r

    for n in range(3):
        dw_zs[n] = summed(pl.ds(lax.rem(zl + n + 1, 4) * 128, 128)).astype(BF)
        d_z(n).start()
    e_z(3).start()
    dw_fin[...] = summed(pl.ds(zl * 128, 128))
    finish(2)
    for n in range(3):
        d_z(n).wait_recv()
    grad = dw_fin[...]
    for n in range(3):
        grad = grad + dw_zr[n].astype(F32)
    dw_sw[...] = grad.astype(BF)

    @pl.when(x != y)
    def _():
        d_swap().start()

    @pl.when(x == y)
    def _():
        dw_gr[...] = dw_sw[...]

    def s_plane(n):
        return send(sq1.at[0], sq1.at[n + 1], s1_s.at[n], s1_r.at[n], at(dx=plane[n][0], dy=plane[n][1]))

    def s_column(n):
        return send(sq2.at[0], sq2.at[n + 1], s2_s.at[n], s2_r.at[n], line(*column[n]))

    squares = jnp.sum((grad * grad).reshape(16, 8, COLS), axis=0)
    sq1[0] = sum(squares[:, b * 128 : b * 128 + 128] for b in range(5))
    for n in range(15):
        s_plane(n).start()
    for n in range(15):
        s_plane(n).wait_recv()
    sq2[0] = jnp.sum(sq1[...], axis=0)
    for n in range(15):
        s_column(n).start()
    for n in range(15):
        s_column(n).wait_recv()
    squared_total = jnp.sum(jnp.sum(sq2[...], axis=0), keepdims=True)
    entries = MODEL_FEATURES * (QUERY_HEADS + 2 * KEY_VALUE_HEADS) * HEAD
    factor = 1.0 / jnp.maximum(jnp.sqrt(squared_total / entries), 1.0)

    @pl.when(x != y)
    def _():
        d_swap().wait()

    vq_ref[...] = 0.9 * mq_ref[...] + factor * dw_gr[:, :384].astype(F32)
    vk_ref[...] = 0.9 * mk_ref[...] + factor * dw_gr[:, 384:512].astype(F32)
    vv_ref[...] = 0.9 * mv_ref[...] + factor * dw_gr[:, 512:].astype(F32)
    finish(3)

    for n in range(3):
        e_y(n).wait()
        x_y(n).wait_send()
        d_x(n).wait_send()
        d_z(n).wait_send()
    for n in range(4):
        x_z(n).wait_send()
        d_core(n).wait_send()
        e_z(n).wait_send()
    for p in range(5):
        for d in range(2):
            g_own(p, d).wait_send()
            g_forward(p, d).wait_send()
    for n in range(15):
        s_plane(n).wait_send()
        s_column(n).wait_send()


def local(*args):
    vm = pltpu.VMEM
    scratch = [
        vm((1024, 1024), BF), vm((2, 512, 1024), BF), vm((4, 2, 128, ALL), BF), vm((2, 512, ALL), BF),
        vm((1024, QB), F32), vm((1024, QB), F32), vm((1024, QB), BF), vm((1024, QB), BF),
        vm((1024, HEAD), F32), vm((1024, HEAD), F32),
        vm((4, 512, COLS), BF), vm((4, 512, COLS), BF), vm((3, 512, COLS), BF), vm((3, 512, COLS), BF),
        vm((512, COLS), F32), vm((3, 128, COLS), BF), vm((3, 128, COLS), BF), vm((128, COLS), F32),
        vm((128, COLS), BF), vm((128, COLS), BF),
        vm((4, 128, 1024), BF), vm((4, 128, 1024), BF), vm((4, 128, 1024), F32), vm((3, 128, 1024), BF),
        vm((16, 8, 128), F32), vm((16, 8, 128), F32),
    ]
    shapes = [(3,), (3,), (3,), (), (3,), (4,), (2, 5), (2, 5), (4,), (3,), (3,), (), (4,), (3,), (15,), (15,)]
    for shape in shapes:
        scratch += [pltpu.SemaphoreType.DMA(shape)] * 2
    whole = pl.BlockSpec(memory_space=pltpu.VMEM)
    return pl.pallas_call(
        kernel,
        out_shape=(
            jax.ShapeDtypeStruct((1, 128, MODEL_FEATURES), BF),
            jax.ShapeDtypeStruct((128, 384), F32),
            jax.ShapeDtypeStruct((128, 128), F32),
            jax.ShapeDtypeStruct((128, 128), F32),
        ),
        in_specs=[whole] * 11,
        out_specs=(whole,) * 4,
        scratch_shapes=scratch,
        compiler_params=pltpu.CompilerParams(
            collective_id=0, has_side_effects=True, vmem_limit_bytes=62 * 1024 * 1024
        ),
        name="block",
    )(*args)


def solution(mesh):
    torus = Mesh(mesh.devices.reshape(4, 4, 2, 4, 2), AXES)
    in_specs = (
        P(DP, TENSOR, None),
        P(DP, None, TENSOR),
        P(DP, None, TENSOR),
        P(DP, None, TENSOR),
        P(DP, None, TENSOR),
        P(DP, TENSOR),
        P(DP, TENSOR),
        P(DP, TENSOR),
        P(DP, TENSOR),
        P(DP, TENSOR),
        P(DP, TENSOR),
    )
    out_specs = (P(DP, TENSOR, None), P(DP, TENSOR), P(DP, TENSOR), P(DP, TENSOR))
    return jax.shard_map(local, mesh=torus, in_specs=in_specs, out_specs=out_specs, check_vma=False)
```

time: 524 us -> 204 us (0.39)
  waiting for transfers between devices: 369 us -> 0 us
  Pallas kernels: 0 us -> 196 us
  blocking collectives: 51.6 us -> 0 us
  matrix products: 41 us -> 0 us
  local copies, waits for them, and re-layouts: 33.3 us -> 4.68 us
  between operations: 15.1 us -> 0.66 us
  other arithmetic: 12.4 us -> 0 us
    reduce_scatter x4 -> x0, waiting for transfers between devices: 200 us -> none  [the longest x2 103 us: summed_rows(): so_far = lax.psum_scatter(so_far, axis, scatter_dimension=0, tiled=True)]
    pallas_call x0 -> x1, Pallas kernels: none -> 196 us  [local(): pl.pallas_call(kernel, out_shape=(jax.ShapeDtypeStruct((1, 128, MODEL_FEA...]
    all_gather x2 -> x0, waiting for transfers between devices: 168 us -> none  [the longest x1 142 us: local(): gathered = lax.all_gather(inputs, TENSOR, axis=1, tiled=True)[0]]
    psum x5 -> x0, blocking collectives: 51.6 us -> none  [over_axes(): return functools.reduce(lax.psum, axes, value)]
    dot_general x12 -> x0, matrix products: 41 us -> none  [the longest x1 11.7 us: local(): lax.dot_general(gathered, local_grads, (((0,), (0,)), ((), ())), preferre...]
    transpose x1 -> x0, local copies, waits for them, and re-layouts: 13.8 us -> none  [scatter_pairs(): parts = parts.reshape(*sizes, *inside).swapaxes(0, 1).reshape(-1, *inside)]
    another operation x1 -> x0, local copies, waits for them, and re-layouts: 9.43 us -> none  [scatter_pairs(): parts = parts.reshape(*sizes, *inside).swapaxes(0, 1).reshape(-1, *inside)]
  transfers between devices with their start and end apart: 6 -> 0, of which waited for: 6 -> 0; matrix products, arithmetic and copies ran while one was open for 16% -> 0% of each run, Pallas kernels for 0% -> 0%
where the time goes in v1:
time: 204 us; the launch traced here: 201 us
  Pallas kernels  196 us (96%)
  local copies, waits for them, and re-layouts  4.68 us (2%)
    pallas_call x1, Pallas kernels, local(): pl.pallas_call(kernel, out_shape=(jax.ShapeDtypeStruct((1, 128, MODEL_FEA...  196 us
    unnamed x10, local copies, waits for them, and re-layouts  4.68 us

profile of v1, /device:TPU:2, one launch (start us, length us, event | category | flops | bytes accessed | tf_op | source)
XLA Modules:
  0.0 200.9 jit_solution(4006759840450190599)
XLA Ops:
  0.6 195.5 %block.1 = (bf16[1,128,4096]{2,1,0:T(8,128)(2,1)}, f32[128,384]{1,0:T(8,128)}, f32[128,128]{1,0:T(8,128)}, f32[128,128]{1,0:T(8,128)}) custom-call(bf16[1,128,4096]{2,1,0:T(8,128)(2,1)} %in_ref.1, bf16[1,1024,384]{2,1,0:T(8,128)(2,1)} %q_ref.1, bf16[1,1024,128]{2,1,0:T(8,128)(2,1)} %k_ref.1, bf16[1,1024,128]{2,1,0:T(8,128)(2,1)} %v_ref.1, ...), custom_call_target="tpu_custom_call" | custom-call | tf_op jit(solution)/shard_map/block/pallas_call | solution.py:397
  196.2 0.0 copy-start
  196.2 2.3 %copy.19 = bf16[1,128,4096]{2,1,0:T(8,128)(2,1)} copy(bf16[1,128,4096]{2,1,0:T(8,128)(2,1)} %get-tuple-element.8) | data formatting | bytes 2097152
  198.5 0.0 copy-done
  198.5 0.0 copy-start.2
  198.5 0.7 copy.20
  199.2 0.2 copy-done.2
  199.4 0.0 copy-start.1
  199.4 0.6 copy.21
  200.0 0.2 copy-done.1
  200.2 0.6 copy.22
Async XLA Ops:
  196.2 2.3 %copy-start = (f32[128,384]{1,0:T(8,128)S(1)}, f32[128,384]{1,0:T(8,128)}, u32[]{:S(2)}) copy-start(f32[128,384]{1,0:T(8,128)} %get-tuple-element.9) | copy-start | bytes 589828
  198.5 0.9 copy-start.2
  199.4 0.9 copy-start.1

commit v2 on v1

--- a/solution.py
+++ b/solution.py
@@ -34,8 +34,9 @@
 
 
 def kernel(
-    in_ref, q_ref, k_ref, v_ref, do_ref, wq_ref, wk_ref, wv_ref, mq_ref, mk_ref, mv_ref,
+    in_ref, q_hbm, k_hbm, v_hbm, do_hbm, wq_ref, wk_ref, wv_ref, mq_hbm, mk_hbm, mv_hbm,
     gx_ref, vq_ref, vk_ref, vv_ref,
+    q_ref, k_ref, v_ref, do_ref, mq_ref, mk_ref, mv_ref, l_sem, lw_sem, lx_sem,
     xq, xt, g, w, s_buf, dp_buf, p_buf, ds_buf, dk_acc, dv_acc,
     dw_cs, dw_cr, dw_xs, dw_xr, dw_acc, dw_zs, dw_zr, dw_fin, dw_sw, dw_gr,
     dx_s, dx_r, dx_o, dx_f, sq1, sq2,
@@ -72,6 +73,17 @@
         pl.semaphore_signal(barrier, inc=1, device_id=at(dx=dx, dy=dy), device_id_type=MESH)
     for dz, dc in column:
         pl.semaphore_signal(barrier, inc=1, device_id=line(dz, dc), device_id_type=MESH)
+    loads = [
+        pltpu.make_async_copy(src, dst, l_sem.at[n])
+        for n, (src, dst) in enumerate(
+            (
+                (q_hbm, q_ref), (k_hbm, k_ref), (v_hbm, v_ref), (do_hbm, do_ref),
+                (mq_hbm, mq_ref), (mk_hbm, mk_ref), (mv_hbm, mv_ref),
+            )
+        )
+    ]
+    for load in loads:
+        load.start()
     pl.semaphore_wait(barrier, 30)
 
     w_rows = pl.ds(zl * 128, 128)
@@ -82,16 +94,21 @@
         dst = w.at[c, w_rows, lanes(y * COLS + off, size)]
         return send(ref, dst, ws_s.at[n], ws_r.at[n], swap_dev)
 
+    def w_here(n):
+        ref, off, size = w_parts[n]
+        return pltpu.make_async_copy(ref, w.at[c, w_rows, lanes(x * COLS + off, size)], lw_sem.at[n])
+
     def w_near(n):
         own = w.at[c, w_rows, lanes(x * COLS, COLS)]
         return send(own, own, wz_s.at[n], wz_r.at[n], at(dl=n + 1))
 
-    def w_far(n):
-        own = w.at[c, :, lanes(x * COLS, COLS)]
-        return send(own, own, wx_s.at[n], wx_r.at[n], at(dx=n + 1))
-
-    def w_core():
-        return send(w.at[c], w.at[c], wc_s, wc_r, core_dev)
+    def w_far(m, n):
+        block = w.at[c, pl.ds(lax.rem(zl + 4 - m, 4) * 128, 128), lanes(x * COLS, COLS)]
+        return send(block, block, wx_s.at[m, n], wx_r.at[m, n], at(dx=n + 1))
+
+    def w_core(n):
+        part = w.at[c, :, lanes(lax.rem(x + 4 - n, 4) * COLS, COLS)]
+        return send(part, part, wc_s.at[n], wc_r.at[n], core_dev)
 
     @pl.when(x != y)
     def _():
@@ -100,8 +117,8 @@
 
     @pl.when(x == y)
     def _():
-        for ref, off, size in w_parts:
-            w[c, w_rows, lanes(x * COLS + off, size)] = ref[...]
+        for n in range(3):
+            w_here(n).start()
 
     def x_rows(dy):
         return pl.ds((2 * lax.rem(y + 4 - dy, 4) + zh) * 128, 128)
@@ -121,7 +138,10 @@
     send(own_x, xq.at[x_rows(0)], xz_s.at[0], xz_r.at[0], zh_dev).start()
     for n in range(3):
         x_y(n).start()
-    xq[x_rows(0), :] = own_x[...]
+    x_here = pltpu.make_async_copy(own_x, xq.at[x_rows(0)], lx_sem)
+    x_here.start()
+    for load in loads[:4]:
+        load.wait()
 
     def g_own(p, d):
         piece = g.at[:, :, :, lanes(y * COLS + p * 128, 128)]
@@ -174,9 +194,6 @@
             dk_acc[:width, :] += dot(ds_buf[:width, :], qi, 1, 0)
             dq = dot(ds_buf[:width, :], k_ref[0, :width, :], 0, 0).astype(BF)
             g[i, :, :, lanes(y * COLS + h * HEAD, HEAD)] = dq.reshape(2, 128, HEAD)
-        g_own(h, 0).start()
-        g_own(h, 1).start()
-
         @pl.when(h == 0)
         def _():
             @pl.when(x != y)
@@ -184,9 +201,18 @@
                 for n in range(3):
                     w_swap(n).wait()
 
+            @pl.when(x == y)
+            def _():
+                for n in range(3):
+                    w_here(n).wait()
+
             for n in range(3):
                 w_near(n).start()
-
+            for n in range(3):
+                w_far(0, n).start()
+
+        g_own(h, 0).start()
+        g_own(h, 1).start()
         return 0
 
     lax.fori_loop(0, 3, head, 0)
@@ -194,14 +220,6 @@
         g[:, :, :, lanes(y * COLS + p * 128, 128)] = acc[...].astype(BF).reshape(4, 2, 128, 128)
         g_own(p, 0).start()
         g_own(p, 1).start()
-    for n in range(3):
-        x_y(n).wait_recv()
-        x_z(n + 1).start()
-    for n in range(3):
-        w_near(n).wait()
-    for n in range(3):
-        w_far(n).start()
-
     def turn(t, _):
         rows = pl.ds(pl.multiple_of(t * 128, 128), 128)
         for b in range(8):
@@ -209,21 +227,38 @@
             xt[b % 2, (b // 2) * 128 : (b // 2) * 128 + 128, lanes(t * 128, 128)] = block.T
         return 0
 
-    for p in range(5):
+    for n in range(3):
+        x_y(n).wait_recv()
+    def forward(p):
         for d in range(2):
             g_own(p, d).wait_recv()
             g_forward(p, d).start()
+
+    def spread(n):
+        w_near(n).wait_recv()
+        for to in range(3):
+            w_far(n + 1, to).start()
+
+    forward(0)
+    for n in range(3):
+        x_z(n + 1).start()
+    forward(1)
+    spread(0)
+    forward(2)
+    spread(1)
+    forward(3)
+    spread(2)
+    forward(4)
+    w_core(0).start()
+    x_here.wait()
     lax.fori_loop(0, 4, lambda b, _: turn(2 * b + zh, 0), 0)
-    for n in range(4):
-        x_z(n).wait_recv()
-    lax.fori_loop(0, 4, lambda b, _: turn(2 * b + other_zh, 0), 0)
-    for n in range(3):
-        w_far(n).wait()
-    w_core().start()
+    for n in range(3):
+        for m in range(4):
+            w_far(m, n).wait_recv()
+        w_core(n + 1).start()
     for p in range(5):
         for d in range(2):
             g_forward(p, d).wait_recv()
-
     def d_core(k):
         return send(dw_cs.at[k], dw_cr.at[k], dc_s.at[k], dc_r.at[k], core_dev)
 
@@ -262,12 +297,10 @@
 
         return 0
 
-    lax.fori_loop(0, 4, for_core, 0)
-    lax.fori_loop(0, 4, for_x, 0)
-
     def e_z(n):
-        to = lax.rem(y + 1 + n, 4)
-        return send(dx_s.at[to], dx_r.at[to], ez_s.at[n], ez_r.at[n], zh_dev)
+        to = lax.rem(y + 1 + min(n, 3), 4)
+        rows = pl.ds(0, 128) if n < 3 else pl.ds((n - 3) * 64, 64)
+        return send(dx_s.at[to, rows], dx_r.at[to, rows], ez_s.at[n], ez_r.at[n], zh_dev)
 
     def e_y(n):
         dst = gx_ref.at[0, :, lanes(y * 1024, 1024)]
@@ -276,13 +309,20 @@
     def back(tokens, half):
         return dot(g[:, tokens].reshape(512, ALL), w[half], 1, 1)
 
-    w_core().wait()
+    for n in range(4):
+        w_core(n).wait()
     for half in range(2):
         r = back(other_zh, half).astype(BF).reshape(4, 128, 512)
         for b in range(4):
             dx_s[:, :, b * 256 + half * 128 : b * 256 + half * 128 + 128] = r[:, :, b * 128 : b * 128 + 128]
-    for n in range(3):
+    for n in range(4):
         e_z(n).start()
+    for n in range(4):
+        x_z(n).wait_recv()
+    lax.fori_loop(0, 4, lambda b, _: turn(2 * b + other_zh, 0), 0)
+    lax.fori_loop(0, 4, for_core, 0)
+    lax.fori_loop(0, 4, for_x, 0)
+
     for half in range(2):
         r = back(zh, half).reshape(4, 128, 512)
         for b in range(4):
@@ -290,6 +330,8 @@
 
     def finish(n):
         e_z(n).wait_recv()
+        if n == 3:
+            e_z(4).wait_recv()
         to = lax.rem(y + 1 + n, 4)
         done = (dx_o[to] + dx_r[to].astype(F32)).astype(BF)
         if n < 3:
@@ -312,7 +354,6 @@
     for n in range(3):
         dw_zs[n] = summed(pl.ds(lax.rem(zl + n + 1, 4) * 128, 128)).astype(BF)
         d_z(n).start()
-    e_z(3).start()
     dw_fin[...] = summed(pl.ds(zl * 128, 128))
     finish(2)
     for n in range(3):
@@ -322,31 +363,33 @@
         grad = grad + dw_zr[n].astype(F32)
     dw_sw[...] = grad.astype(BF)
 
-    @pl.when(x != y)
-    def _():
-        d_swap().start()
-
-    @pl.when(x == y)
-    def _():
-        dw_gr[...] = dw_sw[...]
-
     def s_plane(n):
-        return send(sq1.at[0], sq1.at[n + 1], s1_s.at[n], s1_r.at[n], at(dx=plane[n][0], dy=plane[n][1]))
+        return send(sq2.at[0], sq2.at[n + 1], s2_s.at[n], s2_r.at[n], at(dx=plane[n][0], dy=plane[n][1]))
 
     def s_column(n):
-        return send(sq2.at[0], sq2.at[n + 1], s2_s.at[n], s2_r.at[n], line(*column[n]))
+        return send(sq1.at[0], sq1.at[n + 1], s1_s.at[n], s1_r.at[n], line(*column[n]))
 
     squares = jnp.sum((grad * grad).reshape(16, 8, COLS), axis=0)
     sq1[0] = sum(squares[:, b * 128 : b * 128 + 128] for b in range(5))
-    for n in range(15):
-        s_plane(n).start()
-    for n in range(15):
-        s_plane(n).wait_recv()
-    sq2[0] = jnp.sum(sq1[...], axis=0)
     for n in range(15):
         s_column(n).start()
     for n in range(15):
         s_column(n).wait_recv()
+    sq2[0] = jnp.sum(sq1[...], axis=0)
+    for n in range(15):
+        s_plane(n).start()
+    e_z(4).start()
+
+    @pl.when(x != y)
+    def _():
+        d_swap().start()
+
+    @pl.when(x == y)
+    def _():
+        dw_gr[...] = dw_sw[...]
+
+    for n in range(15):
+        s_plane(n).wait_recv()
     squared_total = jnp.sum(jnp.sum(sq2[...], axis=0), keepdims=True)
     entries = MODEL_FEATURES * (QUERY_HEADS + 2 * KEY_VALUE_HEADS) * HEAD
     factor = 1.0 / jnp.maximum(jnp.sqrt(squared_total / entries), 1.0)
@@ -355,6 +398,8 @@
     def _():
         d_swap().wait()
 
+    for load in loads[4:]:
+        load.wait()
     vq_ref[...] = 0.9 * mq_ref[...] + factor * dw_gr[:, :384].astype(F32)
     vk_ref[...] = 0.9 * mk_ref[...] + factor * dw_gr[:, 384:512].astype(F32)
     vv_ref[...] = 0.9 * mv_ref[...] + factor * dw_gr[:, 512:].astype(F32)
@@ -365,10 +410,14 @@
         x_y(n).wait_send()
         d_x(n).wait_send()
         d_z(n).wait_send()
+        w_near(n).wait_send()
+        for m in range(4):
+            w_far(m, n).wait_send()
     for n in range(4):
         x_z(n).wait_send()
         d_core(n).wait_send()
         e_z(n).wait_send()
+    e_z(4).wait_send()
     for p in range(5):
         for d in range(2):
             g_own(p, d).wait_send()
@@ -381,6 +430,9 @@
 def local(*args):
     vm = pltpu.VMEM
     scratch = [
+        vm((1, 1024, 384), BF), vm((1, 1024, HEAD), BF), vm((1, 1024, HEAD), BF), vm((1, 1024, 384), BF),
+        vm((128, 384), F32), vm((128, HEAD), F32), vm((128, HEAD), F32),
+        pltpu.SemaphoreType.DMA((7,)), pltpu.SemaphoreType.DMA((3,)), pltpu.SemaphoreType.DMA,
         vm((1024, 1024), BF), vm((2, 512, 1024), BF), vm((4, 2, 128, ALL), BF), vm((2, 512, ALL), BF),
         vm((1024, QB), F32), vm((1024, QB), F32), vm((1024, QB), BF), vm((1024, QB), BF),
         vm((1024, HEAD), F32), vm((1024, HEAD), F32),
@@ -390,7 +442,7 @@
         vm((4, 128, 1024), BF), vm((4, 128, 1024), BF), vm((4, 128, 1024), F32), vm((3, 128, 1024), BF),
         vm((16, 8, 128), F32), vm((16, 8, 128), F32),
     ]
-    shapes = [(3,), (3,), (3,), (), (3,), (4,), (2, 5), (2, 5), (4,), (3,), (3,), (), (4,), (3,), (15,), (15,)]
+    shapes = [(3,), (3,), (4, 3), (4,), (3,), (4,), (2, 5), (2, 5), (4,), (3,), (3,), (), (5,), (3,), (15,), (15,)]
     for shape in shapes:
         scratch += [pltpu.SemaphoreType.DMA(shape)] * 2
     whole = pl.BlockSpec(memory_space=pltpu.VMEM)
@@ -402,7 +454,7 @@
             jax.ShapeDtypeStruct((128, 128), F32),
             jax.ShapeDtypeStruct((128, 128), F32),
         ),
-        in_specs=[whole] * 11,
+        in_specs=[pl.BlockSpec(memory_space=pltpu.HBM)] * 11,
         out_specs=(whole,) * 4,
         scratch_shapes=scratch,
         compiler_params=pltpu.CompilerParams(

time: 204 us -> 167 us (0.82); the launches traced: 201 us -> 166 us
  Pallas kernels: 196 us -> 161 us
    pallas_call x1, Pallas kernels: 196 us -> 161 us  [local(): pl.pallas_call(kernel, out_shape=(jax.ShapeDtypeStruct((1, 128, MODEL_FEA...]
where the time goes in v2:
time: 167 us; the launch traced here: 166 us
  Pallas kernels  161 us (96%)
  local copies, waits for them, and re-layouts  4.68 us (3%)
    pallas_call x1, Pallas kernels, local(): pl.pallas_call(kernel, out_shape=(jax.ShapeDtypeStruct((1, 128, MODEL_FEA...  161 us
    unnamed x10, local copies, waits for them, and re-layouts  4.68 us

profile of v2, /device:TPU:2, one launch (start us, length us, event | category | flops | bytes accessed | tf_op | source)
XLA Modules:
  0.0 166.3 jit_solution(16528714017316350743)
XLA Ops:
  0.6 161.0 %block.1 = (bf16[1,128,4096]{2,1,0:T(8,128)(2,1)}, f32[128,384]{1,0:T(8,128)}, f32[128,128]{1,0:T(8,128)}, f32[128,128]{1,0:T(8,128)}) custom-call(bf16[1,128,4096]{2,1,0:T(8,128)(2,1)} %in_ref.1, bf16[1,1024,384]{2,1,0:T(8,128)(2,1)} %q_hbm.1, bf16[1,1024,128]{2,1,0:T(8,128)(2,1)} %k_hbm.1, bf16[1,1024,128]{2,1,0:T(8,128)(2,1)} %v_hbm.1, ...), custom_call_target="tpu_custom_call" | custom-call | tf_op jit(solution)/shard_map/block/pallas_call | solution.py:449
  161.6 0.0 copy-start
  161.6 2.3 %copy.19 = bf16[1,128,4096]{2,1,0:T(8,128)(2,1)} copy(bf16[1,128,4096]{2,1,0:T(8,128)(2,1)} %get-tuple-element.8) | data formatting | bytes 2097152
  163.9 0.0 copy-done
  163.9 0.0 copy-start.2
  163.9 0.7 copy.20
  164.6 0.2 copy-done.2
  164.8 0.0 copy-start.1
  164.8 0.6 copy.21
  165.4 0.2 copy-done.1
  165.7 0.6 copy.22
Async XLA Ops:
  161.6 2.3 %copy-start = (f32[128,384]{1,0:T(8,128)S(1)}, f32[128,384]{1,0:T(8,128)}, u32[]{:S(2)}) copy-start(f32[128,384]{1,0:T(8,128)} %get-tuple-element.9) | copy-start | bytes 589828
  163.9 0.9 copy-start.2
  164.8 0.9 copy-start.1

commit v3 on v2

--- a/solution.py
+++ b/solution.py
@@ -38,11 +38,11 @@
     gx_ref, vq_ref, vk_ref, vv_ref,
     q_ref, k_ref, v_ref, do_ref, mq_ref, mk_ref, mv_ref, l_sem, lw_sem, lx_sem,
     xq, xt, g, w, s_buf, dp_buf, p_buf, ds_buf, dk_acc, dv_acc,
-    dw_cs, dw_cr, dw_xs, dw_xr, dw_acc, dw_zs, dw_zr, dw_fin, dw_sw, dw_gr,
+    dw_cs, dw_cr, dw_xs, dw_xr, dw_vs, dw_vr, dw_h, dw_acc, dw_zs, dw_zr, dw_fin, dw_sw, dw_gr,
     dx_s, dx_r, dx_o, dx_f, sq1, sq2,
     ws_s, ws_r, wz_s, wz_r, wx_s, wx_r, wc_s, wc_r,
     xy_s, xy_r, xz_s, xz_r, go_s, go_r, gf_s, gf_r,
-    dc_s, dc_r, dxx_s, dxx_r, dz_s, dz_r, dsw_s, dsw_r,
+    dc_s, dc_r, dv_s, dv_r, dxx_s, dxx_r, dz_s, dz_r, dsw_s, dsw_r,
     ez_s, ez_r, ey_s, ey_r, s1_s, s1_r, s2_s, s2_r,
 ):
     x, zl, c, y, zh = (lax.axis_index(a) for a in AXES)
@@ -52,6 +52,10 @@
     def at(dx=0, dl=0, dy=0):
         return (lax.rem(x + dx, 4), lax.rem(zl + dl, 4), c, lax.rem(y + dy, 4), zh)
 
+    pair, across = zl + 1 - 2 * lax.rem(zl, 2), lax.rem(zl + 2, 4)
+    blocks = (zl, across, pair, 3 - zl)
+    pair_dev = (x, pair, c, y, zh)
+    across_dev = (x, across, c, y, zh)
     swap_dev = (y, zl, c, x, zh)
     core_dev = (x, zl, other_c, y, zh)
     zh_dev = (x, zl, c, y, other_zh)
@@ -98,13 +102,16 @@
         ref, off, size = w_parts[n]
         return pltpu.make_async_copy(ref, w.at[c, w_rows, lanes(x * COLS + off, size)], lw_sem.at[n])
 
-    def w_near(n):
-        own = w.at[c, w_rows, lanes(x * COLS, COLS)]
-        return send(own, own, wz_s.at[n], wz_r.at[n], at(dl=n + 1))
+    def w_block(m):
+        return w.at[c, pl.ds(blocks[m] * 128, 128), lanes(x * COLS, COLS)]
+
+    def w_near(m):
+        block = w_block((None, 0, 0, 1)[m])
+        dev = across_dev if m == 1 else pair_dev
+        return send(block, block, wz_s.at[m - 1], wz_r.at[m - 1], dev)
 
     def w_far(m, n):
-        block = w.at[c, pl.ds(lax.rem(zl + 4 - m, 4) * 128, 128), lanes(x * COLS, COLS)]
-        return send(block, block, wx_s.at[m, n], wx_r.at[m, n], at(dx=n + 1))
+        return send(w_block(m), w_block(m), wx_s.at[m, n], wx_r.at[m, n], at(dx=n + 1))
 
     def w_core(n):
         part = w.at[c, :, lanes(lax.rem(x + 4 - n, 4) * COLS, COLS)]
@@ -206,8 +213,8 @@
                 for n in range(3):
                     w_here(n).wait()
 
-            for n in range(3):
-                w_near(n).start()
+            w_near(1).start()
+            w_near(2).start()
             for n in range(3):
                 w_far(0, n).start()
 
@@ -220,6 +227,7 @@
         g[:, :, :, lanes(y * COLS + p * 128, 128)] = acc[...].astype(BF).reshape(4, 2, 128, 128)
         g_own(p, 0).start()
         g_own(p, 1).start()
+
     def turn(t, _):
         rows = pl.ds(pl.multiple_of(t * 128, 128), 128)
         for b in range(8):
@@ -227,88 +235,93 @@
             xt[b % 2, (b // 2) * 128 : (b // 2) * 128 + 128, lanes(t * 128, 128)] = block.T
         return 0
 
-    for n in range(3):
-        x_y(n).wait_recv()
     def forward(p):
         for d in range(2):
             g_own(p, d).wait_recv()
             g_forward(p, d).start()
 
-    def spread(n):
-        w_near(n).wait_recv()
-        for to in range(3):
-            w_far(n + 1, to).start()
-
-    forward(0)
+    def spread(m):
+        w_near(m).wait_recv()
+        if m == 1:
+            w_near(3).start()
+        for n in range(3):
+            w_far(m, n).start()
+
+    spread(1)
+    for n in range(3):
+        x_y(n).wait_recv()
+    spread(2)
     for n in range(3):
         x_z(n + 1).start()
+    forward(0)
     forward(1)
-    spread(0)
+    spread(3)
+    w_core(0).start()
     forward(2)
-    spread(1)
     forward(3)
-    spread(2)
     forward(4)
-    w_core(0).start()
     x_here.wait()
     lax.fori_loop(0, 4, lambda b, _: turn(2 * b + zh, 0), 0)
+    def d_core(j):
+        return send(dw_cs.at[j], dw_cr.at[j], dc_s.at[j], dc_r.at[j], core_dev)
+
+    def d_x(d, half):
+        rows = pl.ds(256 * half, 256)
+        return send(
+            dw_xs.at[d, rows], dw_xr.at[d, rows], dxx_s.at[d, half], dxx_r.at[d, half],
+            at(dx=1 if d == 0 else 3),
+        )
+
+    def d_via(d):
+        return send(dw_vs.at[d], dw_vr.at[d], dv_s.at[d], dv_r.at[d], at(dx=1 if d == 0 else 3))
+
+    def d_z(n):
+        dev = across_dev if n == 2 else pair_dev
+        return send(dw_zs.at[n], dw_zr.at[n], dz_s.at[n], dz_r.at[n], dev)
+
+    def d_swap():
+        return send(dw_sw, dw_gr, dsw_s, dsw_r, swap_dev)
+
+    def product(half, k):
+        rhs = g[:, :, :, lanes(k * COLS, COLS)].reshape(1024, COLS)
+        return dot(xt[half], rhs, 1, 0)
+
+    def for_core(j):
+        dw_cs[j] = product(other_c, lax.rem(y + j, 4)).astype(BF)
+        d_core(j).start()
+
+    def for_x(n):
+        k = lax.rem(x + n, 4)
+        j = lax.rem(k + 4 - y, 4)
+        part = product(c, k)
+        d_core(j).wait_recv()
+        return part + dw_cr[j].astype(F32)
+
+    def e_z(n):
+        to = lax.rem(y + 1 + min(n, 3), 4)
+        rows = pl.ds(0, 128) if n < 3 else pl.ds((n - 3) * 64, 64)
+        return send(dx_s.at[to, rows], dx_r.at[to, rows], ez_s.at[n], ez_r.at[n], zh_dev)
+
+    def e_y(n):
+        dst = gx_ref.at[0, :, lanes(y * 1024, 1024)]
+        return send(dx_f.at[n], dst, ey_s.at[n], ey_r.at[n], at(dy=n + 1))
+
+    def back(tokens, half):
+        return dot(g[:, tokens].reshape(512, ALL), w[half], 1, 1)
+
     for n in range(3):
         for m in range(4):
             w_far(m, n).wait_recv()
         w_core(n + 1).start()
+    for n in range(4):
+        x_z(n).wait_recv()
+    lax.fori_loop(0, 4, lambda b, _: turn(2 * b + other_zh, 0), 0)
+    for j in (0, 1, 3):
+        for_core(j)
     for p in range(5):
         for d in range(2):
             g_forward(p, d).wait_recv()
-    def d_core(k):
-        return send(dw_cs.at[k], dw_cr.at[k], dc_s.at[k], dc_r.at[k], core_dev)
-
-    def d_x(n):
-        return send(dw_xs.at[n], dw_xr.at[n], dxx_s.at[n], dxx_r.at[n], at(dx=n + 1))
-
-    def d_z(n):
-        return send(dw_zs.at[n], dw_zr.at[n], dz_s.at[n], dz_r.at[n], at(dl=n + 1))
-
-    def d_swap():
-        return send(dw_sw, dw_gr, dsw_s, dsw_r, swap_dev)
-
-    def product(half, n):
-        k = lax.rem(x + 1 + n, 4)
-        rhs = g[:, :, :, lanes(k * COLS, COLS)].reshape(1024, COLS)
-        return dot(xt[half], rhs, 1, 0)
-
-    def for_core(n, _):
-        dw_cs[n] = product(other_c, n).astype(BF)
-        d_core(n).start()
-        return 0
-
-    def for_x(n, _):
-        part = product(c, n)
-        d_core(n).wait_recv()
-        part = part + dw_cr[n].astype(F32)
-
-        @pl.when(n < 3)
-        def _():
-            dw_xs[n] = part.astype(BF)
-            d_x(n).start()
-
-        @pl.when(n == 3)
-        def _():
-            dw_acc[...] = part
-
-        return 0
-
-    def e_z(n):
-        to = lax.rem(y + 1 + min(n, 3), 4)
-        rows = pl.ds(0, 128) if n < 3 else pl.ds((n - 3) * 64, 64)
-        return send(dx_s.at[to, rows], dx_r.at[to, rows], ez_s.at[n], ez_r.at[n], zh_dev)
-
-    def e_y(n):
-        dst = gx_ref.at[0, :, lanes(y * 1024, 1024)]
-        return send(dx_f.at[n], dst, ey_s.at[n], ey_r.at[n], at(dy=n + 1))
-
-    def back(tokens, half):
-        return dot(g[:, tokens].reshape(512, ALL), w[half], 1, 1)
-
+    for_core(2)
     for n in range(4):
         w_core(n).wait()
     for half in range(2):
@@ -317,12 +330,16 @@
             dx_s[:, :, b * 256 + half * 128 : b * 256 + half * 128 + 128] = r[:, :, b * 128 : b * 128 + 128]
     for n in range(4):
         e_z(n).start()
-    for n in range(4):
-        x_z(n).wait_recv()
-    lax.fori_loop(0, 4, lambda b, _: turn(2 * b + other_zh, 0), 0)
-    lax.fori_loop(0, 4, for_core, 0)
-    lax.fori_loop(0, 4, for_x, 0)
-
+    far = for_x(2)
+    for d in range(2):
+        dw_vs[d] = far[256 * d : 256 * d + 256].astype(BF)
+        d_via(d).start()
+    for d in range(2):
+        near = for_x(1 if d == 0 else 3)
+        dw_xs[d, pl.ds(256 * (1 - d), 256)] = near[256 * (1 - d) : 256 * (1 - d) + 256].astype(BF)
+        d_x(d, 1 - d).start()
+        dw_h[d] = near[256 * d : 256 * d + 256]
+    dw_acc[...] = for_x(0)
     for half in range(2):
         r = back(zh, half).reshape(4, 128, 512)
         for b in range(4):
@@ -340,28 +357,43 @@
         else:
             gx_ref[0, :, lanes(y * 1024, 1024)] = done
 
+    for d in range(2):
+        d_via(d).wait_recv()
+        dw_xs[d, pl.ds(256 * d, 256)] = (dw_h[d] + dw_vr[d].astype(F32)).astype(BF)
+        d_x(d, d).start()
     finish(0)
     finish(1)
-    for n in range(3):
-        d_x(n).wait_recv()
+    for d in range(2):
+        for half in range(2):
+            d_x(d, half).wait_recv()
 
     def summed(rows):
         r = dw_acc[rows, :]
-        for n in range(3):
-            r = r + dw_xr[n, rows, :].astype(F32)
+        for d in range(2):
+            r = r + dw_xr[d, rows, :].astype(F32)
         return r
 
-    for n in range(3):
-        dw_zs[n] = summed(pl.ds(lax.rem(zl + n + 1, 4) * 128, 128)).astype(BF)
+    for n, to in ((1, 3), (0, 2)):
+        dw_zs[n] = summed(pl.ds(blocks[to] * 128, 128)).astype(BF)
         d_z(n).start()
+    rest = summed(pl.ds(across * 128, 128))
+    d_z(1).wait_recv()
+    dw_zs[2] = (rest + dw_zr[1].astype(F32)).astype(BF)
+    d_z(2).start()
     dw_fin[...] = summed(pl.ds(zl * 128, 128))
     finish(2)
-    for n in range(3):
-        d_z(n).wait_recv()
-    grad = dw_fin[...]
-    for n in range(3):
-        grad = grad + dw_zr[n].astype(F32)
+    d_z(0).wait_recv()
+    d_z(2).wait_recv()
+    grad = dw_fin[...] + dw_zr[0].astype(F32) + dw_zr[2].astype(F32)
     dw_sw[...] = grad.astype(BF)
+
+    @pl.when(x != y)
+    def _():
+        d_swap().start()
+
+    @pl.when(x == y)
+    def _():
+        dw_gr[...] = dw_sw[...]
 
     def s_plane(n):
         return send(sq2.at[0], sq2.at[n + 1], s2_s.at[n], s2_r.at[n], at(dx=plane[n][0], dy=plane[n][1]))
@@ -380,14 +412,6 @@
         s_plane(n).start()
     e_z(4).start()
 
-    @pl.when(x != y)
-    def _():
-        d_swap().start()
-
-    @pl.when(x == y)
-    def _():
-        dw_gr[...] = dw_sw[...]
-
     for n in range(15):
         s_plane(n).wait_recv()
     squared_total = jnp.sum(jnp.sum(sq2[...], axis=0), keepdims=True)
@@ -408,9 +432,8 @@
     for n in range(3):
         e_y(n).wait()
         x_y(n).wait_send()
-        d_x(n).wait_send()
         d_z(n).wait_send()
-        w_near(n).wait_send()
+        w_near(n + 1).wait_send()
         for m in range(4):
             w_far(m, n).wait_send()
     for n in range(4):
@@ -418,6 +441,10 @@
         d_core(n).wait_send()
         e_z(n).wait_send()
     e_z(4).wait_send()
+    for d in range(2):
+        d_via(d).wait_send()
+        for half in range(2):
+            d_x(d, half).wait_send()
     for p in range(5):
         for d in range(2):
             g_own(p, d).wait_send()
@@ -436,13 +463,14 @@
         vm((1024, 1024), BF), vm((2, 512, 1024), BF), vm((4, 2, 128, ALL), BF), vm((2, 512, ALL), BF),
         vm((1024, QB), F32), vm((1024, QB), F32), vm((1024, QB), BF), vm((1024, QB), BF),
         vm((1024, HEAD), F32), vm((1024, HEAD), F32),
-        vm((4, 512, COLS), BF), vm((4, 512, COLS), BF), vm((3, 512, COLS), BF), vm((3, 512, COLS), BF),
+        vm((4, 512, COLS), BF), vm((4, 512, COLS), BF), vm((2, 512, COLS), BF), vm((2, 512, COLS), BF),
+        vm((2, 256, COLS), BF), vm((2, 256, COLS), BF), vm((2, 256, COLS), F32),
         vm((512, COLS), F32), vm((3, 128, COLS), BF), vm((3, 128, COLS), BF), vm((128, COLS), F32),
         vm((128, COLS), BF), vm((128, COLS), BF),
         vm((4, 128, 1024), BF), vm((4, 128, 1024), BF), vm((4, 128, 1024), F32), vm((3, 128, 1024), BF),
         vm((16, 8, 128), F32), vm((16, 8, 128), F32),
     ]
-    shapes = [(3,), (3,), (4, 3), (4,), (3,), (4,), (2, 5), (2, 5), (4,), (3,), (3,), (), (5,), (3,), (15,), (15,)]
+    shapes = [(3,), (3,), (4, 3), (4,), (3,), (4,), (2, 5), (2, 5), (4,), (2,), (2, 2), (3,), (), (5,), (3,), (15,), (15,)]
     for shape in shapes:
         scratch += [pltpu.SemaphoreType.DMA(shape)] * 2
     whole = pl.BlockSpec(memory_space=pltpu.VMEM)

time: 167 us -> 155 us (0.928)
  Pallas kernels: 161 us -> 148 us
    pallas_call x1, Pallas kernels: 161 us -> 148 us  [local(): pl.pallas_call(kernel, out_shape=(jax.ShapeDtypeStruct((1, 128, MODEL_FEA...]
where the time goes in v3:
time: 155 us; the launch traced here: 153 us
  Pallas kernels  148 us (95%)
  local copies, waits for them, and re-layouts  4.68 us (3%)
    pallas_call x1, Pallas kernels, local(): pl.pallas_call(kernel, out_shape=(jax.ShapeDtypeStruct((1, 128, MODEL_FEA...  148 us
    unnamed x10, local copies, waits for them, and re-layouts  4.68 us

profile of v3, /device:TPU:2, one launch (start us, length us, event | category | flops | bytes accessed | tf_op | source)
XLA Modules:
  0.0 153.0 jit_solution(12224243086454291607)
XLA Ops:
  0.6 147.7 %block.1 = (bf16[1,128,4096]{2,1,0:T(8,128)(2,1)}, f32[128,384]{1,0:T(8,128)}, f32[128,128]{1,0:T(8,128)}, f32[128,128]{1,0:T(8,128)}) custom-call(bf16[1,128,4096]{2,1,0:T(8,128)(2,1)} %in_ref.1, bf16[1,1024,384]{2,1,0:T(8,128)(2,1)} %q_hbm.1, bf16[1,1024,128]{2,1,0:T(8,128)(2,1)} %k_hbm.1, bf16[1,1024,128]{2,1,0:T(8,128)(2,1)} %v_hbm.1, ...), custom_call_target="tpu_custom_call" | custom-call | tf_op jit(solution)/shard_map/block/pallas_call | solution.py:477
  148.3 0.0 copy-start
  148.3 2.3 %copy.19 = bf16[1,128,4096]{2,1,0:T(8,128)(2,1)} copy(bf16[1,128,4096]{2,1,0:T(8,128)(2,1)} %get-tuple-element.8) | data formatting | bytes 2097152
  150.7 0.0 copy-done
  150.7 0.0 copy-start.2
  150.7 0.7 copy.20
  151.3 0.2 copy-done.2
  151.5 0.0 copy-start.1
  151.5 0.6 copy.21
  152.2 0.2 copy-done.1
  152.4 0.6 copy.22
Async XLA Ops:
  148.3 2.3 %copy-start = (f32[128,384]{1,0:T(8,128)S(1)}, f32[128,384]{1,0:T(8,128)}, u32[]{:S(2)}) copy-start(f32[128,384]{1,0:T(8,128)} %get-tuple-element.9) | copy-start | bytes 589828
  150.7 0.9 copy-start.2
  151.5 0.9 copy-start.1

commit v4 on v3

--- a/solution.py
+++ b/solution.py
@@ -150,14 +150,14 @@
     for load in loads[:4]:
         load.wait()
 
-    def g_own(p, d):
-        piece = g.at[:, :, :, lanes(y * COLS + p * 128, 128)]
-        return send(piece, piece, go_s.at[d, p], go_r.at[d, p], at(dy=1 if d == 0 else 3))
-
-    def g_forward(p, d):
+    def g_own(t, p, d):
+        piece = g.at[:, (other_zh, zh)[t], :, lanes(y * COLS + p * 128, 128)]
+        return send(piece, piece, go_s.at[t, d, p], go_r.at[t, d, p], at(dy=1 if d == 0 else 3))
+
+    def g_forward(t, p, d):
         of = lax.rem(y + (3 if d == 0 else 1), 4)
-        half = g.at[2 * d : 2 * d + 2, :, :, lanes(of * COLS + p * 128, 128)]
-        return send(half, half, gf_s.at[d, p], gf_r.at[d, p], at(dy=1 if d == 0 else 3))
+        half = g.at[2 * d : 2 * d + 2, (other_zh, zh)[t], :, lanes(of * COLS + p * 128, 128)]
+        return send(half, half, gf_s.at[t, d, p], gf_r.at[t, d, p], at(dy=1 if d == 0 else 3))
 
     dk_acc[...] = jnp.zeros_like(dk_acc)
     dv_acc[...] = jnp.zeros_like(dv_acc)
@@ -218,15 +218,15 @@
             for n in range(3):
                 w_far(0, n).start()
 
-        g_own(h, 0).start()
-        g_own(h, 1).start()
+        g_own(0, h, 0).start()
+        g_own(0, h, 1).start()
         return 0
 
     lax.fori_loop(0, 3, head, 0)
     for p, acc in ((3, dk_acc), (4, dv_acc)):
         g[:, :, :, lanes(y * COLS + p * 128, 128)] = acc[...].astype(BF).reshape(4, 2, 128, 128)
-        g_own(p, 0).start()
-        g_own(p, 1).start()
+        g_own(0, p, 0).start()
+        g_own(0, p, 1).start()
 
     def turn(t, _):
         rows = pl.ds(pl.multiple_of(t * 128, 128), 128)
@@ -235,10 +235,10 @@
             xt[b % 2, (b // 2) * 128 : (b // 2) * 128 + 128, lanes(t * 128, 128)] = block.T
         return 0
 
-    def forward(p):
+    def forward(t, p):
         for d in range(2):
-            g_own(p, d).wait_recv()
-            g_forward(p, d).start()
+            g_own(t, p, d).wait_recv()
+            g_forward(t, p, d).start()
 
     def spread(m):
         w_near(m).wait_recv()
@@ -253,13 +253,13 @@
     spread(2)
     for n in range(3):
         x_z(n + 1).start()
-    forward(0)
-    forward(1)
+    for p in range(5):
+        forward(0, p)
+    for p in range(5):
+        for d in range(2):
+            g_own(1, p, d).start()
     spread(3)
     w_core(0).start()
-    forward(2)
-    forward(3)
-    forward(4)
     x_here.wait()
     lax.fori_loop(0, 4, lambda b, _: turn(2 * b + zh, 0), 0)
     def d_core(j):
@@ -297,22 +297,37 @@
         d_core(j).wait_recv()
         return part + dw_cr[j].astype(F32)
 
-    def e_z(n):
-        to = lax.rem(y + 1 + min(n, 3), 4)
-        rows = pl.ds(0, 128) if n < 3 else pl.ds((n - 3) * 64, 64)
-        return send(dx_s.at[to, rows], dx_r.at[to, rows], ez_s.at[n], ez_r.at[n], zh_dev)
-
-    def e_y(n):
-        dst = gx_ref.at[0, :, lanes(y * 1024, 1024)]
-        return send(dx_f.at[n], dst, ey_s.at[n], ey_r.at[n], at(dy=n + 1))
+    def e_z(q):
+        to, rows = lax.rem(y + 1 + q // 2, 4), pl.ds((q % 2) * 64, 64)
+        return send(dx_s.at[to, rows], dx_r.at[to, rows], ez_s.at[q], ez_r.at[q], zh_dev)
+
+    def e_y(q):
+        rows = pl.ds((q % 2) * 64, 64)
+        dst = gx_ref.at[0, rows, lanes(y * 1024, 1024)]
+        return send(dx_f.at[q // 2, rows], dst, ey_s.at[q], ey_r.at[q], at(dy=q // 2 + 1))
 
     def back(tokens, half):
         return dot(g[:, tokens].reshape(512, ALL), w[half], 1, 1)
 
+    for p in range(3):
+        forward(1, p)
     for n in range(3):
         for m in range(4):
             w_far(m, n).wait_recv()
         w_core(n + 1).start()
+    forward(1, 3)
+    forward(1, 4)
+    for p in range(5):
+        for d in range(2):
+            g_forward(0, p, d).wait_recv()
+    for n in range(4):
+        w_core(n).wait()
+    for half in range(2):
+        r = back(other_zh, half).astype(BF).reshape(4, 128, 512)
+        for b in range(4):
+            dx_s[:, :, b * 256 + half * 128 : b * 256 + half * 128 + 128] = r[:, :, b * 128 : b * 128 + 128]
+    for q in range(4):
+        e_z(q).start()
     for n in range(4):
         x_z(n).wait_recv()
     lax.fori_loop(0, 4, lambda b, _: turn(2 * b + other_zh, 0), 0)
@@ -320,16 +335,8 @@
         for_core(j)
     for p in range(5):
         for d in range(2):
-            g_forward(p, d).wait_recv()
+            g_forward(1, p, d).wait_recv()
     for_core(2)
-    for n in range(4):
-        w_core(n).wait()
-    for half in range(2):
-        r = back(other_zh, half).astype(BF).reshape(4, 128, 512)
-        for b in range(4):
-            dx_s[:, :, b * 256 + half * 128 : b * 256 + half * 128 + 128] = r[:, :, b * 128 : b * 128 + 128]
-    for n in range(4):
-        e_z(n).start()
     far = for_x(2)
     for d in range(2):
         dw_vs[d] = far[256 * d : 256 * d + 256].astype(BF)
@@ -345,24 +352,24 @@
         for b in range(4):
             dx_o[:, :, b * 256 + half * 128 : b * 256 + half * 128 + 128] = r[:, :, b * 128 : b * 128 + 128]
 
-    def finish(n):
-        e_z(n).wait_recv()
-        if n == 3:
-            e_z(4).wait_recv()
-        to = lax.rem(y + 1 + n, 4)
-        done = (dx_o[to] + dx_r[to].astype(F32)).astype(BF)
-        if n < 3:
-            dx_f[n] = done
-            e_y(n).start()
+    def finish(q):
+        e_z(q).wait_recv()
+        to, rows = lax.rem(y + 1 + q // 2, 4), pl.ds((q % 2) * 64, 64)
+        done = (dx_o[to, rows] + dx_r[to, rows].astype(F32)).astype(BF)
+        if q < 6:
+            dx_f[q // 2, rows] = done
+            e_y(q).start()
         else:
-            gx_ref[0, :, lanes(y * 1024, 1024)] = done
+            gx_ref[0, rows, lanes(y * 1024, 1024)] = done
 
     for d in range(2):
         d_via(d).wait_recv()
         dw_xs[d, pl.ds(256 * d, 256)] = (dw_h[d] + dw_vr[d].astype(F32)).astype(BF)
         d_x(d, d).start()
-    finish(0)
-    finish(1)
+    e_z(4).start()
+    e_z(5).start()
+    for q in range(4):
+        finish(q)
     for d in range(2):
         for half in range(2):
             d_x(d, half).wait_recv()
@@ -381,7 +388,8 @@
     dw_zs[2] = (rest + dw_zr[1].astype(F32)).astype(BF)
     d_z(2).start()
     dw_fin[...] = summed(pl.ds(zl * 128, 128))
-    finish(2)
+    finish(4)
+    finish(5)
     d_z(0).wait_recv()
     d_z(2).wait_recv()
     grad = dw_fin[...] + dw_zr[0].astype(F32) + dw_zr[2].astype(F32)
@@ -405,12 +413,13 @@
     sq1[0] = sum(squares[:, b * 128 : b * 128 + 128] for b in range(5))
     for n in range(15):
         s_column(n).start()
+    e_z(6).start()
+    e_z(7).start()
     for n in range(15):
         s_column(n).wait_recv()
     sq2[0] = jnp.sum(sq1[...], axis=0)
     for n in range(15):
         s_plane(n).start()
-    e_z(4).start()
 
     for n in range(15):
         s_plane(n).wait_recv()
@@ -427,10 +436,10 @@
     vq_ref[...] = 0.9 * mq_ref[...] + factor * dw_gr[:, :384].astype(F32)
     vk_ref[...] = 0.9 * mk_ref[...] + factor * dw_gr[:, 384:512].astype(F32)
     vv_ref[...] = 0.9 * mv_ref[...] + factor * dw_gr[:, 512:].astype(F32)
-    finish(3)
+    finish(6)
+    finish(7)
 
     for n in range(3):
-        e_y(n).wait()
         x_y(n).wait_send()
         d_z(n).wait_send()
         w_near(n + 1).wait_send()
@@ -439,16 +448,19 @@
     for n in range(4):
         x_z(n).wait_send()
         d_core(n).wait_send()
-        e_z(n).wait_send()
-    e_z(4).wait_send()
+    for q in range(8):
+        e_z(q).wait_send()
+    for q in range(6):
+        e_y(q).wait()
     for d in range(2):
         d_via(d).wait_send()
         for half in range(2):
             d_x(d, half).wait_send()
     for p in range(5):
         for d in range(2):
-            g_own(p, d).wait_send()
-            g_forward(p, d).wait_send()
+            for t in range(2):
+                g_own(t, p, d).wait_send()
+                g_forward(t, p, d).wait_send()
     for n in range(15):
         s_plane(n).wait_send()
         s_column(n).wait_send()
@@ -470,7 +482,7 @@
         vm((4, 128, 1024), BF), vm((4, 128, 1024), BF), vm((4, 128, 1024), F32), vm((3, 128, 1024), BF),
         vm((16, 8, 128), F32), vm((16, 8, 128), F32),
     ]
-    shapes = [(3,), (3,), (4, 3), (4,), (3,), (4,), (2, 5), (2, 5), (4,), (2,), (2, 2), (3,), (), (5,), (3,), (15,), (15,)]
+    shapes = [(3,), (3,), (4, 3), (4,), (3,), (4,), (2, 2, 5), (2, 2, 5), (4,), (2,), (2, 2), (3,), (), (8,), (6,), (15,), (15,)]
     for shape in shapes:
         scratch += [pltpu.SemaphoreType.DMA(shape)] * 2
     whole = pl.BlockSpec(memory_space=pltpu.VMEM)
@@ -486,7 +498,7 @@
         out_specs=(whole,) * 4,
         scratch_shapes=scratch,
         compiler_params=pltpu.CompilerParams(
-            collective_id=0, has_side_effects=True, vmem_limit_bytes=62 * 1024 * 1024
+            collective_id=0, has_side_effects=True, vmem_limit_bytes=53 * 1024 * 1024 + 768 * 1024
         ),
         name="block",
     )(*args)

time: 155 us -> 147 us (0.948)
  Pallas kernels: 148 us -> 140 us
    pallas_call x1, Pallas kernels: 148 us -> 140 us  [local(): pl.pallas_call(kernel, out_shape=(jax.ShapeDtypeStruct((1, 128, MODEL_FEA...]
where the time goes in v4:
time: 147 us; the launch traced here: 146 us
  Pallas kernels  140 us (95%)
  local copies, waits for them, and re-layouts  5.77 us (4%)
    pallas_call x1, Pallas kernels, local(): pl.pallas_call(kernel, out_shape=(jax.ShapeDtypeStruct((1, 128, MODEL_FEA...  140 us
    unnamed x10, local copies, waits for them, and re-layouts  5.77 us

profile of v4, /device:TPU:2, one launch (start us, length us, event | category | flops | bytes accessed | tf_op | source)
XLA Modules:
  0.0 146.1 jit_solution(2007685547589909445)
XLA Ops:
  0.6 0.0 copy-start
  0.6 0.7 copy-done
  1.4 0.0 copy-start.1
  1.4 0.8 copy-done.1
  2.2 139.7 %block.1 = (bf16[1,128,4096]{2,1,0:T(8,128)(2,1)}, f32[128,384]{1,0:T(8,128)}, f32[128,128]{1,0:T(8,128)S(1)}, f32[128,128]{1,0:T(8,128)S(1)}) custom-call(bf16[1,128,4096]{2,1,0:T(8,128)(2,1)} %in_ref.1, bf16[1,1024,384]{2,1,0:T(8,128)(2,1)} %q_hbm.1, bf16[1,1024,128]{2,1,0:T(8,128)(2,1)} %k_hbm.1, bf16[1,1024,128]{2,1,0:T(8,128)(2,1)} %v_hbm.1, ...), custom_call_target="tpu_custom_call" | custom-call | tf_op jit(solution)/shard_map/block/pallas_call | solution.py:489
  141.8 0.0 copy-start.2
  141.8 2.3 %copy.19 = bf16[1,128,4096]{2,1,0:T(8,128)(2,1)} copy(bf16[1,128,4096]{2,1,0:T(8,128)(2,1)} %get-tuple-element.8) | data formatting | bytes 2097152
  144.2 0.0 copy-done.2
  144.2 0.7 copy.20
  144.8 0.6 copy.21
  145.5 0.6 copy.22
Async XLA Ops:
  0.6 0.8 copy-start
  1.4 0.8 copy-start.1
  141.8 2.3 %copy-start.2 = (f32[128,384]{1,0:T(8,128)S(1)}, f32[128,384]{1,0:T(8,128)}, u32[]{:S(2)}) copy-start(f32[128,384]{1,0:T(8,128)} %get-tuple-element.9) | copy-start | bytes 589828

commit v5 on v4

--- a/solution.py
+++ b/solution.py
@@ -414,12 +414,12 @@
     for n in range(15):
         s_column(n).start()
     e_z(6).start()
-    e_z(7).start()
     for n in range(15):
         s_column(n).wait_recv()
     sq2[0] = jnp.sum(sq1[...], axis=0)
     for n in range(15):
         s_plane(n).start()
+    e_z(7).start()
 
     for n in range(15):
         s_plane(n).wait_recv()

time: 147 us -> 145 us (0.986)
  the two profiles are of different devices: /device:TPU:2 before, /device:TPU:57 now
where the time goes in v5:
time: 145 us
  Pallas kernels  138 us (95%)
  local copies, waits for them, and re-layouts  5.77 us (4%)
    pallas_call x1, Pallas kernels, local(): pl.pallas_call(kernel, out_shape=(jax.ShapeDtypeStruct((1, 128, MODEL_FEA...  138 us
    unnamed x10, local copies, waits for them, and re-layouts  5.77 us

profile of v5, /device:TPU:57, one launch (start us, length us, event | category | flops | bytes accessed | tf_op | source)
XLA Modules:
  0.0 144.6 jit_solution(4244415570459593735)
XLA Ops:
  0.6 0.0 copy-start
  0.6 0.7 copy-done
  1.4 0.0 copy-start.1
  1.4 0.8 copy-done.1
  2.2 138.2 %block.1 = (bf16[1,128,4096]{2,1,0:T(8,128)(2,1)}, f32[128,384]{1,0:T(8,128)}, f32[128,128]{1,0:T(8,128)S(1)}, f32[128,128]{1,0:T(8,128)S(1)}) custom-call(bf16[1,128,4096]{2,1,0:T(8,128)(2,1)} %in_ref.1, bf16[1,1024,384]{2,1,0:T(8,128)(2,1)} %q_hbm.1, bf16[1,1024,128]{2,1,0:T(8,128)(2,1)} %k_hbm.1, bf16[1,1024,128]{2,1,0:T(8,128)(2,1)} %v_hbm.1, ...), custom_call_target="tpu_custom_call" | custom-call | tf_op jit(solution)/shard_map/block/pallas_call | solution.py:489
  140.3 0.0 copy-start.2
  140.4 2.3 %copy.19 = bf16[1,128,4096]{2,1,0:T(8,128)(2,1)} copy(bf16[1,128,4096]{2,1,0:T(8,128)(2,1)} %get-tuple-element.8) | data formatting | bytes 2097152
  142.7 0.0 copy-done.2
  142.7 0.7 copy.20
  143.4 0.6 copy.21
  144.0 0.6 copy.22
Async XLA Ops:
  0.6 0.8 copy-start
  1.4 0.8 copy-start.1
  140.3 2.3 %copy-start.2 = (f32[128,384]{1,0:T(8,128)S(1)}, f32[128,384]{1,0:T(8,128)}, u32[]{:S(2)}) copy-start(f32[128,384]{1,0:T(8,128)} %get-tuple-element.9) | copy-start | bytes 589828
